TPU v7x, 32 devices: a whole 2x2x4 slice. The times are simulated.
32 devices in a mesh: gy: 8 (over z, y), gz: 4 (over x, core).
Axes of the slice: x: 2, y: 2, z: 4, core: 2. Of those that a mesh axis runs over, the one named last changes fastest.
Arguments:
- tokens: bfloat16 [2, 64, 8, 8, 1024], P(None, None, 'gy', 'gz'), may hold values from -64 to 64
- w_qkv: bfloat16 [1024, 3072], P('gy'), may hold values from -2 to 2
- w_out: bfloat16 [1024, 1024], P('gy'), may hold values from -0.1875 to 0.1875
- bias_x: float32 [16, 127], replicated, may hold values from -4 to 4
- bias_y: float32 [16, 15], replicated, may hold values from -4 to 4
- bias_z: float32 [16, 15], replicated, may hold values from -4 to 4
Outputs:
- mixed: bfloat16 [2, 64, 8, 8, 1024], P(None, None, 'gy', 'gz')
All inputs are finite; a program needn't handle non-finite values.
Results may differ from a plain program's by a relative error of at most 0.0083.
Values may be sent and summed in bfloat16 or wider, within the bound.
A program may use at most 64 MiB of HBM per device.

v0:
```python
import jax
import jax.numpy as jnp
from jax import lax
from jax.sharding import PartitionSpec as P

HEADS = 16
HEAD = 64
einsum_forms = {
    1: ("bxyzhs,bwyzhs->byzhxw", "byzhxw,bwyzhs->bxyzhs"),
    2: ("bxyzhs,bxwzhs->bxzhyw", "bxzhyw,bxwzhs->bxyzhs"),
    3: ("bxyzhs,bxywhs->bxyhzw", "bxyhzw,bxywhs->bxyzhs"),
}


def norm_rows(tokens):
    values = tokens.astype(jnp.float32)
    center = jnp.mean(values, axis=-1, keepdims=True)
    spread = jnp.mean((values - center) ** 2, axis=-1, keepdims=True)
    return ((values - center) * lax.rsqrt(spread + 1e-05)).astype(jnp.bfloat16)


def rel_bias(table):
    length = (table.shape[1] + 1) // 2
    offsets = (
        lax.broadcasted_iota(jnp.int32, (length, length), 0)
        - lax.broadcasted_iota(jnp.int32, (length, length), 1)
        + length
        - 1
    )
    lookup = (
        offsets[:, :, None] == lax.broadcasted_iota(jnp.int32, (1, 1, 2 * length - 1), 2)
    ).astype(jnp.float32)
    return jnp.einsum("hr,ijr->hij", table, lookup, precision=lax.Precision.HIGHEST)


def attend(qkv, table, axis):
    dims = qkv.shape
    features = dims[-1] // 3
    parts = qkv.reshape(dims[:-1] + (3, HEADS, HEAD))
    query = parts[..., 0, :, :]
    keys = parts[..., 1, :, :]
    values = parts[..., 2, :, :]
    score_form, mix_form = einsum_forms[axis]
    scores = jnp.einsum(score_form, query, keys, preferred_element_type=jnp.float32) * HEAD ** (
        -0.5
    ) + rel_bias(table)
    scores = scores - jnp.max(scores, axis=-1, keepdims=True)
    expo = jnp.exp(scores)
    weights = (expo / jnp.sum(expo, axis=-1, keepdims=True)).astype(jnp.bfloat16)
    mixed = jnp.einsum(mix_form, weights, values, preferred_element_type=jnp.float32)
    return mixed.reshape(dims[:-1] + (features,)).astype(jnp.bfloat16)


def return_y(result):
    return lax.all_to_all(result, "gy", split_axis=2, concat_axis=1, tiled=True)


def return_z(result):
    return lax.all_to_all(result, "gz", split_axis=3, concat_axis=1, tiled=True)


def shards(tokens, w_qkv, w_out, bias_x, bias_y, bias_z):
    samples, depth, rows_y, rows_z, features = tokens.shape
    normed = norm_rows(tokens)
    gathered = lax.all_gather(w_qkv, "gy", axis=0, tiled=True)

    def project(inputs):
        product = jnp.dot(
            inputs.reshape(-1, features), gathered, preferred_element_type=jnp.float32
        )
        return product.astype(jnp.bfloat16).reshape(inputs.shape[:-1] + (3 * features,))

    along_x = attend(project(normed), bias_x, 1)
    along_y = return_y(
        attend(
            project(lax.all_to_all(normed, "gy", split_axis=1, concat_axis=2, tiled=True)),
            bias_y,
            2,
        )
    )
    along_z = return_z(
        attend(
            project(lax.all_to_all(normed, "gz", split_axis=1, concat_axis=3, tiled=True)),
            bias_z,
            3,
        )
    )
    summed = along_x.astype(jnp.float32) + along_y.astype(jnp.float32) + along_z.astype(jnp.float32)
    summed = summed.astype(jnp.bfloat16).reshape(-1, features)
    residual = tokens.reshape(-1, features).astype(jnp.float32)
    result = residual + jnp.dot(
        summed, lax.all_gather(w_out, "gy", axis=0, tiled=True), preferred_element_type=jnp.float32
    )
    return result.astype(jnp.bfloat16).reshape(tokens.shape)


def solution(mesh):
    placed = (P(None, None, "gy", "gz", None), P("gy", None), P("gy", None), P(), P(), P())
    return jax.shard_map(
        shards,
        mesh=mesh,
        in_specs=placed,
        out_specs=P(None, None, "gy", "gz", None),
        check_vma=False,
    )
```

profile of v0, /device:TPU:0, one launch (start us, length us, event | category | flops | bytes accessed | tf_op | source)
XLA Modules:
  0.0 212.9 jit_solution(13488122357055576503)
XLA Ops:
  6.5 0.7 all-gather.3.cloned.1.call-update
  7.3 1.6 convert_reduce_fusion
  8.9 0.0 copy-start.11
  8.9 1.9 multiply_reduce_fusion
  10.8 0.1 add_rsqrt_fusion
  10.9 0.0 copy-start.12
  10.9 1.4 multiply_convert_fusion
  12.3 4.2 %all-to-all-start.2 = ((bf16[2,64,1,2,1024]{4,3,2,0,1:T(2,128)(2,1)}), bf16[2,64,1,2,1024]{4,3,2,0,1:T(2,128)(2,1)S(1)}, u32[]{:S(2)}, u32[]{:S(2)}) async-start(bf16[2,64,1,2,1024]{4,3,2,0,1:T(2,128)(2,1)} %multiply_convert_fusion), calls=%async_computation.2 | async-start | bytes 1048576 | tf_op jit(solution)/shard_map/all_to_all | solution.py:83
  16.6 0.7 all-gather.5.cloned.1.call-update
  17.3 8.1 %all-to-all-done.2 = bf16[2,64,1,2,1024]{4,3,2,0,1:T(2,128)(2,1)S(1)} async-done(((bf16[2,64,1,2,1024]{4,3,2,0,1:T(2,128)(2,1)}), bf16[2,64,1,2,1024]{4,3,2,0,1:T(2,128)(2,1)S(1)}, u32[]{:S(2)}, u32[]{:S(2)}) %all-to-all-start.2) | async-done | bytes 524320 | tf_op jit(solution)/shard_map/all_to_all | solution.py:83
  25.4 6.5 %all-to-all-start = ((bf16[2,64,1,2,1024]{4,3,2,0,1:T(2,128)(2,1)}), bf16[2,64,1,2,1024]{4,3,2,0,1:T(2,128)(2,1)S(1)}, u32[]{:S(2)}, u32[]{:S(2)}) async-start(bf16[2,64,1,2,1024]{4,3,2,0,1:T(2,128)(2,1)} %multiply_convert_fusion), calls=%async_computation | async-start | bytes 1048576 | tf_op jit(solution)/shard_map/all_to_all | solution.py:76
  31.9 0.2 convolution_bitcast_fusion.1
  32.1 1.4 copy.77
  33.5 0.1 copy.88
  33.6 0.2 convolution_bitcast_fusion
  33.8 0.1 copy.97
  33.9 1.0 reshape.177
  35.0 3.2 %fusion.11 = f32[16,64,64]{2,0,1:T(8,128)S(1)} fusion(s32[64,64]{1,0:T(8,128)S(1)} %subtract_add_fusion, f32[16,127]{1,0:T(8,128)S(1)} %copy-done), kind=kOutput, calls=%fused_computation.29 | convolution fusion | flops 100397056 | bytes 286656 | tf_op jit(solution)/shard_map/hr,ijr->hij/dot_general | solution.py:33
  38.1 1.1 copy.81
  39.2 0.6 copy_convert_fusion
  39.8 0.1 copy.76
  39.9 1.7 reshape.187
  41.6 0.5 copy.174
  42.2 0.2 reshape.182
  42.4 17.7 %all-to-all-done = bf16[2,64,1,2,1024]{4,3,2,0,1:T(2,128)(2,1)S(1)} async-done(((bf16[2,64,1,2,1024]{4,3,2,0,1:T(2,128)(2,1)}), bf16[2,64,1,2,1024]{4,3,2,0,1:T(2,128)(2,1)S(1)}, u32[]{:S(2)}, u32[]{:S(2)}) %all-to-all-start) | async-done | bytes 524320 | tf_op jit(solution)/shard_map/all_to_all | solution.py:76
  60.1 0.5 copy.175
  60.5 1.0 reshape.181
  61.5 60.6 %all-gather.3.cloned.1.call-done = bf16[1024,3072]{1,0:T(8,128)(2,1)} async-done(((bf16[128,3072]{1,0:T(8,128)(2,1)}), bf16[1024,3072]{1,0:T(8,128)(2,1)}) %all-gather.3.cloned.1.call-update) | async-done | bytes 6291472 | tf_op jit(solution)/shard_map/all_gather | solution.py:65
  122.1 5.8 %convolution_convert_fusion = bf16[256,3072]{1,0:T(8,128)(2,1)} fusion(bf16[256,1024]{1,0:T(8,128)(2,1)S(1)} %reshape.182, bf16[1024,3072]{1,0:T(8,128)(2,1)} %all-gather.3.cloned.1.call-done), kind=kOutput, calls=%fused_computation.3 | convolution fusion | flops 1611399168 | bytes 8388608 | tf_op jit(solution)/shard_map/dot_general | solution.py:68
  127.9 3.6 %reshape_reshape.11 = bf16[2,16,1,8,3,16,64]{6,5,4,3,1,0,2:T(8,128)(2,1)S(1)} reshape(bf16[256,3072]{1,0:T(8,128)(2,1)} %convolution_convert_fusion) | data formatting | bytes 3145728 | tf_op jit(solution)/shard_map/reshape;reshape | solution.py:39
  131.6 0.0 copy-start.10
  131.6 2.1 fusion.36
  133.7 5.9 %convolution_convert_fusion.1 = bf16[256,3072]{1,0:T(8,128)(2,1)} fusion(bf16[256,1024]{1,0:T(8,128)(2,1)S(1)} %copy-done.10, bf16[1024,3072]{1,0:T(8,128)(2,1)} %all-gather.3.cloned.1.call-done), kind=kOutput, calls=%fused_computation.4 | convolution fusion | flops 1611399168 | bytes 8388608 | tf_op jit(solution)/shard_map/dot_general | solution.py:68
  139.6 3.0 %fusion.37 = (f32[2,16,16,8]{3,2,1,0:T(8,128)S(1)}, f32[2,16,16,8,8]{3,4,2,1,0:T(8,128)}) fusion(f32[16,8,8]{1,2,0:T(8,128)S(1)} %copy.97, bf16[2,16,1,8,1,16,64]{6,5,4,3,1,0,2:T(8,128)(2,1)S(1)} %copy-done.8, bf16[2,16,1,8,1,16,64]{6,5,4,3,1,0,2:T(8,128)(2,1)S(1)} %copy-done.7), kind=kOutput, calls=%fused_computation.79 | convolution fusion | flops 4325383 | bytes 1200128 | tf_op jit(solution)/shard_map/sub | solution.py:47
  142.7 3.6 %reshape_reshape.10 = bf16[2,8,8,2,3,16,64]{6,5,4,3,2,1,0:T(8,128)(2,1)S(1)} reshape(bf16[256,3072]{1,0:T(8,128)(2,1)} %convolution_convert_fusion.1) | data formatting | bytes 3145728 | tf_op jit(solution)/shard_map/reshape;reshape | solution.py:39
  146.3 2.7 %fusion.9 = bf16[2,16,1,8,16,64]{5,3,4,1,0,2:T(8,128)(2,1)S(1)} fusion(f32[2,16,16,8,8]{3,4,2,1,0:T(8,128)} %get-tuple-element.15, bf16[2,16,1,8,1,16,64]{6,5,4,3,1,0,2:T(8,128)(2,1)} %get-tuple-element.11, f32[2,16,16,8]{3,2,1,0:T(8,128)S(1)} %get-tuple-element.14), kind=kOutput, calls=%fused_computation.26 | convolution fusion | flops 4521984 | bytes 1196032 | tf_op jit(solution)/shard_map/bxyhzw,bxywhs->bxyzhs/dot_general | solution.py:50
  149.1 1.3 copy.108
  150.4 2.6 %reshape.198 = bf16[2,16,1,8,1024]{4,1,0,2,3:T(8,128)(2,1)} reshape(bf16[2,16,1,8,16,64]{5,4,1,0,3,2:T(8,128)(2,1)} %copy.108) | data formatting | bytes 1048576 | tf_op jit(solution)/shard_map/convert_element_type | solution.py:51
  153.0 4.4 %all-to-all-start.3 = ((bf16[2,16,1,8,1024]{4,1,0,2,3:T(8,128)(2,1)}), bf16[2,16,1,8,1024]{4,1,0,2,3:T(8,128)(2,1)}, u32[]{:S(2)}, u32[]{:S(2)}) async-start(bf16[2,16,1,8,1024]{4,1,0,2,3:T(8,128)(2,1)} %reshape.198), calls=%async_computation.3 | async-start | bytes 1048576 | tf_op jit(solution)/shard_map/all_to_all | solution.py:59
  157.3 2.2 %fusion.34 = (bf16[2,8,8,2,1,16,64]{6,5,4,3,2,1,0:T(8,128)(2,1)}, bf16[2,8,8,2,1,16,64]{6,5,4,3,2,1,0:T(8,128)(2,1)}, bf16[2,8,8,2,1,16,64]{6,5,4,3,2,1,0:T(8,128)(2,1)}) fusion(bf16[2,8,8,2,3,16,64]{6,5,4,3,2,1,0:T(8,128)(2,1)S(1)} %reshape_reshape.10), kind=kLoop, calls=%fused_computation.76 | loop fusion | bytes 3145728 | tf_op jit(solution)/shard_map/slice | solution.py:42
  159.6 3.4 %fusion.39 = (f32[2,8,2,16,8]{4,3,2,1,0:T(8,128)S(1)}, f32[2,8,2,16,8,8]{4,5,3,2,1,0:T(8,128)S(1)}) fusion(f32[16,8,8]{1,2,0:T(8,128)S(1)} %copy.88, bf16[2,8,8,2,1,16,64]{6,5,4,3,2,1,0:T(8,128)(2,1)} %get-tuple-element.7, bf16[2,8,8,2,1,16,64]{6,5,4,3,2,1,0:T(8,128)(2,1)} %get-tuple-element.6), kind=kOutput, calls=%fused_computation.81 | convolution fusion | flops 4325383 | bytes 1200128 | tf_op jit(solution)/shard_map/sub | solution.py:47
  163.0 6.0 %convolution_convert_fusion.2 = bf16[256,3072]{1,0:T(8,128)(2,1)} fusion(bf16[256,1024]{1,0:T(8,128)(2,1)S(1)} %copy-done.9, bf16[1024,3072]{1,0:T(8,128)(2,1)} %all-gather.3.cloned.1.call-done), kind=kOutput, calls=%fused_computation.5 | convolution fusion | flops 1611399168 | bytes 8388608 | tf_op jit(solution)/shard_map/dot_general | solution.py:68
  168.9 0.9 fusion.8
  169.9 0.2 copy.107
  170.1 1.4 reshape.197
  171.5 3.6 %reshape_reshape.9 = bf16[2,64,1,2,3,16,64]{6,5,4,3,1,0,2:T(8,128)(2,1)S(1)} reshape(bf16[256,3072]{1,0:T(8,128)(2,1)} %convolution_convert_fusion.2) | data formatting | bytes 3145728 | tf_op jit(solution)/shard_map/reshape;reshape | solution.py:39
  175.1 1.9 fusion.35
  177.0 2.3 %copy.111 = bf16[2,64,1,2,1,16,64]{1,6,5,3,0,4,2:T(8,128)(2,1)S(1)} copy(bf16[2,64,1,2,1,16,64]{6,5,4,3,1,0,2:T(8,128)(2,1)} %get-tuple-element.8) | data formatting | bytes 1048576
  179.4 0.0 all-to-all-done.3
  179.4 4.4 %all-to-all-start.1 = ((bf16[2,8,8,2,1024]{4,3,1,0,2:T(2,128)(2,1)}), bf16[2,8,8,2,1024]{4,3,1,0,2:T(2,128)(2,1)}, u32[]{:S(2)}, u32[]{:S(2)}) async-start(bf16[2,8,8,2,1024]{4,3,1,0,2:T(2,128)(2,1)} %reshape.197), calls=%async_computation.1 | async-start | bytes 1048576 | tf_op jit(solution)/shard_map/all_to_all | solution.py:55
  183.8 3.7 %fusion.38 = (f32[2,2,16,64]{3,2,1,0:T(8,128)S(1)}, f32[2,2,16,64,64]{3,4,2,1,0:T(8,128)}) fusion(f32[16,64,64]{1,2,0:T(8,128)} %copy.81, bf16[2,64,1,2,1,16,64]{6,5,4,3,1,0,2:T(8,128)(2,1)S(1)} %copy-done.4, bf16[2,64,1,2,1,16,64]{6,5,4,3,1,0,2:T(8,128)(2,1)S(1)} %copy-done.5), kind=kOutput, calls=%fused_computation.80 | convolution fusion | flops 34603072 | bytes 2375680 | tf_op jit(solution)/shard_map/sub | solution.py:47
  187.5 3.4 %convert_bitcast_fusion = f32[2,64,1,2,16,64]{1,5,4,3,0,2:T(8,128)} fusion(f32[2,2,16,64,64]{3,4,2,1,0:T(8,128)} %get-tuple-element.17, bf16[2,64,1,2,1,16,64]{1,6,5,3,0,4,2:T(8,128)(2,1)S(1)} %copy.111, f32[2,2,16,64]{3,2,1,0:T(8,128)S(1)} %get-tuple-element.16), kind=kOutput, calls=%fused_computation.6 | convolution fusion | flops 34603008 | bytes 2637824 | tf_op jit(solution)/shard_map/byzhxw,bwyzhs->bxyzhs/dot_general | solution.py:50
  190.9 3.1 %copy.83 = f32[2,64,1,2,16,64]{5,4,3,1,0,2:T(8,128)S(1)} copy(f32[2,64,1,2,16,64]{1,5,4,3,0,2:T(8,128)} %convert_bitcast_fusion) | data formatting | bytes 2097152 | tf_op jit(solution)/shard_map/convert_element_type | solution.py:88
  194.0 0.6 reshape.188
  194.5 1.1 copy.101
  195.6 0.1 convert_bitcast_fusion.1
  195.7 0.8 copy.102
  196.6 1.8 reshape.190
  198.3 0.3 all-to-all-done.1
  198.7 1.5 convert_bitcast_fusion.2
  200.2 0.1 copy.92
  200.2 1.7 reshape.189
  201.9 3.1 %fusion.10 = bf16[256,1024]{1,0:T(8,128)(2,1)S(1)} fusion(f32[256,1024]{1,0:T(8,128)S(1)} %copy-done.3, bf16[1024,1024]{1,0:T(8,128)(2,1)} %all-gather.5.cloned.1.call-done, f32[256,1024]{1,0:T(8,128)} %reshape.190, f32[256,1024]{1,0:T(8,128)S(1)} %reshape.188, f32[256,1024]{1,0:T(8,128)} %reshape.189), kind=kOutput, calls=%fused_computation.28 | convolution fusion | flops 538181632 | bytes 6815744 | tf_op jit(solution)/shard_map/dot_general | solution.py:91
  205.0 1.0 reshape.186
  (29 shorter events, 0.1 us)
Async XLA Ops:
  6.5 28.4 %copy-start = (f32[16,127]{1,0:T(8,128)S(1)}, f32[16,127]{1,0:T(8,128)}, u32[]{:S(2)}) copy-start(f32[16,127]{1,0:T(8,128)} %param.9) | copy-start | bytes 24388
  6.5 4.3 %copy-start.2 = (bf16[2,64,1,2,1024]{4,3,2,1,0:T(2,128)(2,1)S(1)}, bf16[2,64,1,2,1024]{4,3,2,1,0:T(2,128)(2,1)}, u32[]{:S(2)}) copy-start(bf16[2,64,1,2,1024]{4,3,2,1,0:T(2,128)(2,1)} %param.6) | copy-start | bytes 1572868
  6.5 115.6 %all-gather.3.cloned.1.call-start = ((), (), s32[]{:S(2)}) async-start(), calls=%async_computation.4 | async-start | bytes 7077888 | tf_op jit(solution)/shard_map/all_gather | solution.py:65
  8.9 23.0 %copy-start.11 = (f32[16,15]{1,0:T(8,128)S(1)}, f32[16,15]{1,0:T(8,128)}, u32[]{:S(2)}) copy-start(f32[16,15]{1,0:T(8,128)} %param.10) | copy-start | bytes 2884
  10.9 22.7 %copy-start.12 = (f32[16,15]{1,0:T(8,128)S(1)}, f32[16,15]{1,0:T(8,128)}, u32[]{:S(2)}) copy-start(f32[16,15]{1,0:T(8,128)} %param.11) | copy-start | bytes 2884
  12.3 13.1 %all-to-all-start.2 = ((bf16[2,64,1,2,1024]{4,3,2,0,1:T(2,128)(2,1)}), bf16[2,64,1,2,1024]{4,3,2,0,1:T(2,128)(2,1)S(1)}, u32[]{:S(2)}, u32[]{:S(2)}) async-start(bf16[2,64,1,2,1024]{4,3,2,0,1:T(2,128)(2,1)} %multiply_convert_fusion), calls=%async_computation.2 | async-start | bytes 1048576 | tf_op jit(solution)/shard_map/all_to_all | solution.py:83
  16.6 185.4 %all-gather.5.cloned.1.call-start = ((), (), s32[]{:S(2)}) async-start(), calls=%async_computation.5 | async-start | bytes 2359296 | tf_op jit(solution)/shard_map/all_gather | solution.py:92
  25.4 34.7 %all-to-all-start = ((bf16[2,64,1,2,1024]{4,3,2,0,1:T(2,128)(2,1)}), bf16[2,64,1,2,1024]{4,3,2,0,1:T(2,128)(2,1)S(1)}, u32[]{:S(2)}, u32[]{:S(2)}) async-start(bf16[2,64,1,2,1024]{4,3,2,0,1:T(2,128)(2,1)} %multiply_convert_fusion), calls=%async_computation | async-start | bytes 1048576 | tf_op jit(solution)/shard_map/all_to_all | solution.py:76
  131.6 2.1 %copy-start.10 = (bf16[256,1024]{1,0:T(8,128)(2,1)S(1)}, bf16[256,1024]{1,0:T(8,128)(2,1)}, u32[]{:S(2)}) copy-start(bf16[256,1024]{1,0:T(8,128)(2,1)} %reshape.181) | copy-start | bytes 1572868
  133.7 5.9 %copy-start.7 = (bf16[2,16,1,8,1,16,64]{6,5,4,3,1,0,2:T(8,128)(2,1)S(1)}, bf16[2,16,1,8,1,16,64]{6,5,4,3,1,0,2:T(8,128)(2,1)}, u32[]{:S(2)}) copy-start(bf16[2,16,1,8,1,16,64]{6,5,4,3,1,0,2:T(8,128)(2,1)} %get-tuple-element.12) | copy-start | bytes 1572868
  133.7 5.9 %copy-start.8 = (bf16[2,16,1,8,1,16,64]{6,5,4,3,1,0,2:T(8,128)(2,1)S(1)}, bf16[2,16,1,8,1,16,64]{6,5,4,3,1,0,2:T(8,128)(2,1)}, u32[]{:S(2)}) copy-start(bf16[2,16,1,8,1,16,64]{6,5,4,3,1,0,2:T(8,128)(2,1)} %get-tuple-element.13) | copy-start | bytes 1572868
  153.0 26.4 %all-to-all-start.3 = ((bf16[2,16,1,8,1024]{4,1,0,2,3:T(8,128)(2,1)}), bf16[2,16,1,8,1024]{4,1,0,2,3:T(8,128)(2,1)}, u32[]{:S(2)}, u32[]{:S(2)}) async-start(bf16[2,16,1,8,1024]{4,1,0,2,3:T(8,128)(2,1)} %reshape.198), calls=%async_computation.3 | async-start | bytes 1048576 | tf_op jit(solution)/shard_map/all_to_all | solution.py:59
  159.6 3.4 %copy-start.9 = (bf16[256,1024]{1,0:T(8,128)(2,1)S(1)}, bf16[256,1024]{1,0:T(8,128)(2,1)}, u32[]{:S(2)}) copy-start(bf16[256,1024]{1,0:T(8,128)(2,1)} %reshape.177) | copy-start | bytes 1572868
  163.0 6.0 %copy-start.6 = (bf16[2,8,8,2,1,16,64]{6,5,4,3,2,1,0:T(8,128)(2,1)S(1)}, bf16[2,8,8,2,1,16,64]{6,5,4,3,2,1,0:T(8,128)(2,1)}, u32[]{:S(2)}) copy-start(bf16[2,8,8,2,1,16,64]{6,5,4,3,2,1,0:T(8,128)(2,1)} %get-tuple-element.5) | copy-start | bytes 1572868
  177.0 6.8 %copy-start.4 = (bf16[2,64,1,2,1,16,64]{6,5,4,3,1,0,2:T(8,128)(2,1)S(1)}, bf16[2,64,1,2,1,16,64]{6,5,4,3,1,0,2:T(8,128)(2,1)}, u32[]{:S(2)}) copy-start(bf16[2,64,1,2,1,16,64]{6,5,4,3,1,0,2:T(8,128)(2,1)} %get-tuple-element.9) | copy-start | bytes 1572868
  177.0 6.8 %copy-start.5 = (bf16[2,64,1,2,1,16,64]{6,5,4,3,1,0,2:T(8,128)(2,1)S(1)}, bf16[2,64,1,2,1,16,64]{6,5,4,3,1,0,2:T(8,128)(2,1)}, u32[]{:S(2)}) copy-start(bf16[2,64,1,2,1,16,64]{6,5,4,3,1,0,2:T(8,128)(2,1)} %get-tuple-element.10) | copy-start | bytes 1572868
  179.4 19.3 %all-to-all-start.1 = ((bf16[2,8,8,2,1024]{4,3,1,0,2:T(2,128)(2,1)}), bf16[2,8,8,2,1024]{4,3,1,0,2:T(2,128)(2,1)}, u32[]{:S(2)}, u32[]{:S(2)}) async-start(bf16[2,8,8,2,1024]{4,3,1,0,2:T(2,128)(2,1)} %reshape.197), calls=%async_computation.1 | async-start | bytes 1048576 | tf_op jit(solution)/shard_map/all_to_all | solution.py:55
  200.2 1.8 copy-start.3
  201.9 4.1 %copy-start.1 = (f32[16,127]{1,0:T(8,128)S(1)}, f32[16,127]{1,0:T(8,128)}, u32[]{:S(2)}) copy-start(f32[16,127]{1,0:T(8,128)} %param.9) | copy-start | bytes 24388
Sparse Core Ops, SparseCore 0:
  9.5 112.5 all-gather.2
  124.3 47.2 all-gather.4
where the time goes:
time: 214 us; the launch traced here: 213 us
  waiting for transfers between devices  88.1 us (41%)
  local copies, waits for them, and re-layouts  42.8 us (20%)
  matrix products  41.5 us (19%)
  starting transfers between devices  19.5 us (9%)
  between operations  13.7 us (6%)
  other arithmetic  7.17 us (3%)
    all_gather x1, waiting for transfers between devices, shards(): gathered = lax.all_gather(w_qkv, 'gy', axis=0, tiled=True)  60.6 us
    all_to_all x1, waiting for transfers between devices, shards(): lax.all_to_all(normed, 'gy', split_axis=1, concat_axis=2, tiled=True)  17.7 us
    dot_general x3, matrix products, project(): jnp.dot(inputs.reshape(-1, features), gathered, preferred_element_type=jn...  17.7 us
    another operation x3, local copies, waits for them, and re-layouts, attend(): parts = qkv.reshape(dims[:-1] + (3, HEADS, HEAD))  10.9 us
    sub x3, matrix products, attend(): scores = scores - jnp.max(scores, axis=-1, keepdims=True)  10.1 us
    all_to_all x1, waiting for transfers between devices, shards(): lax.all_to_all(normed, 'gz', split_axis=1, concat_axis=3, tiled=True)  8.07 us
    dot_general x3, matrix products, attend(): jnp.einsum(mix_form, weights, values, preferred_element_type=jnp.float32)  7.03 us
    all_to_all x1, starting transfers between devices, shards(): lax.all_to_all(normed, 'gy', split_axis=1, concat_axis=2, tiled=True)  6.52 us
  transfers between devices with their start and end apart: 6, of which 4 were waited for; matrix products, arithmetic and copies ran while one was open for 41% of the time, Pallas kernels for 0%

commit v1 on v0

--- a/solution.py
+++ b/solution.py
@@ -62,7 +62,10 @@
 def shards(tokens, w_qkv, w_out, bias_x, bias_y, bias_z):
     samples, depth, rows_y, rows_z, features = tokens.shape
     normed = norm_rows(tokens)
-    gathered = lax.all_gather(w_qkv, "gy", axis=0, tiled=True)
+    n_dev = lax.axis_size("gy")
+    blocks = jnp.stack([w_qkv for _ in range(n_dev)])
+    blocks = lax.all_to_all(blocks, "gy", split_axis=0, concat_axis=0)
+    gathered = jnp.concatenate(blocks, axis=0)
 
     def project(inputs):
         product = jnp.dot(

time: 214 us -> 309 us (1.44)
  waiting for transfers between devices: 88.1 us -> 153 us
  blocking collectives: 0 us -> 32.6 us
  starting transfers between devices: 19.5 us -> 13.9 us
    all_to_all x2 -> x1, waiting for transfers between devices: 25.7 us -> 152 us  [shards(): blocks = lax.all_to_all(blocks, 'gy', split_axis=0, concat_axis=0)]
    all_gather x1 -> x0, waiting for transfers between devices: 60.6 us -> none  [shards(): gathered = lax.all_gather(w_qkv, 'gy', axis=0, tiled=True)]
    all_to_all x0 -> x2, blocking collectives: none -> 32.6 us  [the longest x1 19.7 us: shards(): lax.all_to_all(normed, 'gy', split_axis=1, concat_axis=2, tiled=True)]
    all_to_all x2 -> x1, starting transfers between devices: 10.8 us -> 4.89 us  [shards(): blocks = lax.all_to_all(blocks, 'gy', split_axis=0, concat_axis=0)]
    another operation x0 -> x1, local copies, waits for them, and re-layouts: none -> 3.45 us  [shards(): blocks = jnp.stack([w_qkv for _ in range(n_dev)])]
  transfers between devices with their start and end apart: 6 -> 4, of which waited for: 4 -> 2; matrix products, arithmetic and copies ran while one was open for 41% -> 27% of each run, Pallas kernels for 0% -> 0%
where the time goes in v1:
time: 309 us; the launch traced here: 308 us
  waiting for transfers between devices  153 us (50%)
  local copies, waits for them, and re-layouts  44.4 us (14%)
  matrix products  42.8 us (14%)
  blocking collectives  32.6 us (11%)
  starting transfers between devices  13.9 us (4%)
  between operations  13.8 us (4%)
  other arithmetic  7.47 us (2%)
    all_to_all x1, waiting for transfers between devices, shards(): blocks = lax.all_to_all(blocks, 'gy', split_axis=0, concat_axis=0)  152 us
    all_to_all x1, blocking collectives, shards(): lax.all_to_all(normed, 'gy', split_axis=1, concat_axis=2, tiled=True)  19.7 us
    dot_general x3, matrix products, project(): jnp.dot(inputs.reshape(-1, features), gathered, preferred_element_type=jn...  17.4 us
    all_to_all x1, blocking collectives, shards(): lax.all_to_all(normed, 'gz', split_axis=1, concat_axis=3, tiled=True)  12.9 us
    sub x3, matrix products, attend(): scores = scores - jnp.max(scores, axis=-1, keepdims=True)  11.6 us
    another operation x3, local copies, waits for them, and re-layouts, attend(): parts = qkv.reshape(dims[:-1] + (3, HEADS, HEAD))  10.9 us
    dot_general x3, matrix products, attend(): jnp.einsum(mix_form, weights, values, preferred_element_type=jnp.float32)  7.02 us
    slice x3, local copies, waits for them, and re-layouts, attend(): values = parts[..., 2, :, :]  6.37 us
  transfers between devices with their start and end apart: 4, of which 2 were waited for; matrix products, arithmetic and copies ran while one was open for 27% of the time, Pallas kernels for 0%

profile of v1, /device:TPU:0, one launch (start us, length us, event | category | flops | bytes accessed | tf_op | source)
XLA Modules:
  0.0 307.5 jit_solution(5048563156827702463)
XLA Ops:
  6.5 1.6 convert_reduce_fusion
  8.1 0.0 copy-start.7
  8.2 2.0 multiply_reduce_fusion
  10.1 0.1 add_rsqrt_fusion
  10.2 1.7 multiply_convert_fusion
  11.9 12.9 %all_to_all.53 = bf16[2,64,1,2,1024]{4,3,2,0,1:T(2,128)(2,1)S(1)} all-to-all(bf16[2,64,1,2,1024]{4,3,2,0,1:T(2,128)(2,1)S(1)} %multiply_convert_fusion), channel_id=1, replica_groups=mesh['gy'=8,'gz'=4] {'gz'}, dimensions={1} | all-to-all | bytes 1048576 | tf_op jit(solution)/shard_map/all_to_all | solution.py:86
  24.7 19.7 %all_to_all.54 = bf16[2,64,1,2,1024]{4,3,2,0,1:T(2,128)(2,1)S(1)} all-to-all(bf16[2,64,1,2,1024]{4,3,2,0,1:T(2,128)(2,1)S(1)} %multiply_convert_fusion), channel_id=1, replica_groups=mesh['gy'=8,'gz'=4] {'gy'}, dimensions={1} | all-to-all | bytes 1048576 | tf_op jit(solution)/shard_map/all_to_all | solution.py:79
  44.5 3.4 %stack.2 = bf16[8,128,3072]{2,1,0:T(8,128)(2,1)} broadcast(bf16[128,3072]{1,0:T(8,128)(2,1)S(1)} %copy-done.7), dimensions={1,2} | broadcast | bytes 7077888 | tf_op jit(solution)/shard_map/stack | solution.py:66
  47.9 4.9 %all-to-all-start = ((bf16[8,128,3072]{2,1,0:T(8,128)(2,1)}), bf16[8,128,3072]{2,1,0:T(8,128)(2,1)}, u32[]{:S(2)}, u32[]{:S(2)}) async-start(bf16[8,128,3072]{2,1,0:T(8,128)(2,1)} %stack.2), calls=%async_computation | async-start | bytes 12582912 | tf_op jit(solution)/shard_map/all_to_all | solution.py:67
  52.8 0.2 all-gather.2.cloned.1.call-start
  53.0 0.5 all-gather.2.cloned.1.call-update
  53.6 0.0 copy-start.2
  53.6 0.4 copy.77
  54.0 0.2 convolution_bitcast_fusion.1
  54.2 0.1 copy.88
  54.3 0.2 convolution_bitcast_fusion
  54.5 0.1 copy.97
  54.6 1.0 reshape.182
  55.6 0.0 copy-done
  55.6 3.2 %fusion.11 = f32[16,64,64]{2,0,1:T(8,128)S(1)} fusion(s32[64,64]{1,0:T(8,128)S(1)} %subtract_add_fusion, f32[16,127]{1,0:T(8,128)S(1)} %copy-done), kind=kOutput, calls=%fused_computation.29 | convolution fusion | flops 100397056 | bytes 286656 | tf_op jit(solution)/shard_map/hr,ijr->hij/dot_general | solution.py:33
  58.8 1.1 copy.81
  59.9 0.6 copy_convert_fusion
  60.5 0.1 copy.76
  60.5 1.7 reshape.193
  62.3 0.5 copy.174
  62.8 0.2 reshape.188
  63.0 0.5 copy.175
  63.5 0.2 reshape.187
  63.7 151.6 %all-to-all-done = bf16[8,128,3072]{2,1,0:T(8,128)(2,1)} async-done(((bf16[8,128,3072]{2,1,0:T(8,128)(2,1)}), bf16[8,128,3072]{2,1,0:T(8,128)(2,1)}, u32[]{:S(2)}, u32[]{:S(2)}) %all-to-all-start) | async-done | bytes 6291488 | tf_op jit(solution)/shard_map/all_to_all | solution.py:67
  215.3 5.8 %convolution_convert_fusion.1 = bf16[256,3072]{1,0:T(8,128)(2,1)} fusion(bf16[256,1024]{1,0:T(8,128)(2,1)S(1)} %reshape.187, bf16[1024,3072]{1,0:T(8,128)(2,1)} %bitcast), kind=kOutput, calls=%fused_computation.4 | convolution fusion | flops 1611399168 | bytes 8388608 | tf_op jit(solution)/shard_map/dot_general | solution.py:71
  221.2 5.8 %convolution_convert_fusion = bf16[256,3072]{1,0:T(8,128)(2,1)} fusion(bf16[256,1024]{1,0:T(8,128)(2,1)S(1)} %reshape.188, bf16[1024,3072]{1,0:T(8,128)(2,1)} %bitcast), kind=kOutput, calls=%fused_computation.3 | convolution fusion | flops 1611399168 | bytes 8388608 | tf_op jit(solution)/shard_map/dot_general | solution.py:71
  226.9 3.6 %reshape_reshape.11 = bf16[2,16,1,8,3,16,64]{6,5,4,3,1,0,2:T(8,128)(2,1)S(1)} reshape(bf16[256,3072]{1,0:T(8,128)(2,1)} %convolution_convert_fusion) | data formatting | bytes 3145728 | tf_op jit(solution)/shard_map/reshape;reshape | solution.py:39
  230.6 2.2 fusion.36
  232.7 4.6 %fusion.37 = (f32[2,16,16,8]{3,2,1,0:T(8,128)S(1)}, f32[2,16,16,8,8]{3,4,2,1,0:T(8,128)}) fusion(f32[16,8,8]{1,2,0:T(8,128)S(1)} %copy.97, bf16[2,16,1,8,1,16,64]{6,5,4,3,1,0,2:T(8,128)(2,1)} %get-tuple-element.13, bf16[2,16,1,8,1,16,64]{6,5,4,3,1,0,2:T(8,128)(2,1)} %get-tuple-element.12), kind=kOutput, calls=%fused_computation.79 | convolution fusion | flops 4325383 | bytes 1200128 | tf_op jit(solution)/shard_map/sub | solution.py:47
  237.3 3.6 %reshape_reshape.10 = bf16[2,8,8,2,3,16,64]{6,5,4,3,2,1,0:T(8,128)(2,1)S(1)} reshape(bf16[256,3072]{1,0:T(8,128)(2,1)} %convolution_convert_fusion.1) | data formatting | bytes 3145728 | tf_op jit(solution)/shard_map/reshape;reshape | solution.py:39
  241.0 2.7 fusion.9
  243.7 1.2 copy.108
  244.9 2.6 reshape.204
  247.5 4.4 %all-to-all-start.4 = ((bf16[2,16,1,8,1024]{4,1,0,2,3:T(8,128)(2,1)}), bf16[2,16,1,8,1024]{4,1,0,2,3:T(8,128)(2,1)}, u32[]{:S(2)}, u32[]{:S(2)}) async-start(bf16[2,16,1,8,1024]{4,1,0,2,3:T(8,128)(2,1)} %reshape.204), calls=%async_computation.4 | async-start | bytes 1048576 | tf_op jit(solution)/shard_map/all_to_all | solution.py:59
  251.9 2.2 fusion.34
  254.1 3.4 %fusion.39 = (f32[2,8,2,16,8]{4,3,2,1,0:T(8,128)S(1)}, f32[2,8,2,16,8,8]{4,5,3,2,1,0:T(8,128)S(1)}) fusion(f32[16,8,8]{1,2,0:T(8,128)S(1)} %copy.88, bf16[2,8,8,2,1,16,64]{6,5,4,3,2,1,0:T(8,128)(2,1)} %get-tuple-element.7, bf16[2,8,8,2,1,16,64]{6,5,4,3,2,1,0:T(8,128)(2,1)} %get-tuple-element.6), kind=kOutput, calls=%fused_computation.81 | convolution fusion | flops 4325383 | bytes 1200128 | tf_op jit(solution)/shard_map/sub | solution.py:47
  257.6 5.8 %convolution_convert_fusion.2 = bf16[256,3072]{1,0:T(8,128)(2,1)} fusion(bf16[256,1024]{1,0:T(8,128)(2,1)S(1)} %copy-done.8, bf16[1024,3072]{1,0:T(8,128)(2,1)} %bitcast), kind=kOutput, calls=%fused_computation.5 | convolution fusion | flops 1611399168 | bytes 8388608 | tf_op jit(solution)/shard_map/dot_general | solution.py:71
  263.4 0.9 fusion.8
  264.3 0.2 copy.107
  264.5 1.4 reshape.203
  265.9 3.6 %reshape_reshape.9 = bf16[2,64,1,2,3,16,64]{6,5,4,3,1,0,2:T(8,128)(2,1)S(1)} reshape(bf16[256,3072]{1,0:T(8,128)(2,1)} %convolution_convert_fusion.2) | data formatting | bytes 3145728 | tf_op jit(solution)/shard_map/reshape;reshape | solution.py:39
  269.6 2.0 fusion.35
  271.6 2.3 copy.111
  273.9 0.0 all-to-all-done.4
  273.9 4.4 %all-to-all-start.2 = ((bf16[2,8,8,2,1024]{4,3,1,0,2:T(2,128)(2,1)}), bf16[2,8,8,2,1024]{4,3,1,0,2:T(2,128)(2,1)}, u32[]{:S(2)}, u32[]{:S(2)}) async-start(bf16[2,8,8,2,1024]{4,3,1,0,2:T(2,128)(2,1)} %reshape.203), calls=%async_computation.2 | async-start | bytes 1048576 | tf_op jit(solution)/shard_map/all_to_all | solution.py:55
  278.4 3.7 %fusion.38 = (f32[2,2,16,64]{3,2,1,0:T(8,128)S(1)}, f32[2,2,16,64,64]{3,4,2,1,0:T(8,128)}) fusion(f32[16,64,64]{1,2,0:T(8,128)} %copy.81, bf16[2,64,1,2,1,16,64]{6,5,4,3,1,0,2:T(8,128)(2,1)S(1)} %copy-done.4, bf16[2,64,1,2,1,16,64]{6,5,4,3,1,0,2:T(8,128)(2,1)S(1)} %copy-done.5), kind=kOutput, calls=%fused_computation.80 | convolution fusion | flops 34603072 | bytes 2375680 | tf_op jit(solution)/shard_map/sub | solution.py:47
  282.0 3.4 %convert_bitcast_fusion = f32[2,64,1,2,16,64]{1,5,4,3,0,2:T(8,128)} fusion(f32[2,2,16,64,64]{3,4,2,1,0:T(8,128)} %get-tuple-element.17, bf16[2,64,1,2,1,16,64]{1,6,5,3,0,4,2:T(8,128)(2,1)S(1)} %copy.111, f32[2,2,16,64]{3,2,1,0:T(8,128)S(1)} %get-tuple-element.16), kind=kOutput, calls=%fused_computation.6 | convolution fusion | flops 34603008 | bytes 2637824 | tf_op jit(solution)/shard_map/byzhxw,bwyzhs->bxyzhs/dot_general | solution.py:50
  285.4 3.1 %copy.83 = f32[2,64,1,2,16,64]{5,4,3,1,0,2:T(8,128)S(1)} copy(f32[2,64,1,2,16,64]{1,5,4,3,0,2:T(8,128)} %convert_bitcast_fusion) | data formatting | bytes 2097152 | tf_op jit(solution)/shard_map/convert_element_type | solution.py:91
  288.5 0.6 reshape.194
  289.1 1.1 copy.101
  290.2 0.1 convert_bitcast_fusion.1
  290.3 0.8 copy.102
  291.1 1.7 reshape.196
  292.8 0.5 all-to-all-done.2
  293.3 1.5 convert_bitcast_fusion.2
  294.8 0.1 copy.92
  294.8 1.7 reshape.195
  296.6 3.1 %fusion.10 = bf16[256,1024]{1,0:T(8,128)(2,1)S(1)} fusion(f32[256,1024]{1,0:T(8,128)S(1)} %copy-done.3, bf16[1024,1024]{1,0:T(8,128)(2,1)} %all-gather.2.cloned.1.call-done, f32[256,1024]{1,0:T(8,128)} %reshape.196, f32[256,1024]{1,0:T(8,128)S(1)} %reshape.194, f32[256,1024]{1,0:T(8,128)} %reshape.195), kind=kOutput, calls=%fused_computation.28 | convolution fusion | flops 538181632 | bytes 6815744 | tf_op jit(solution)/shard_map/dot_general | solution.py:94
  299.7 1.0 reshape.192
  (23 shorter events, 0.1 us)
Async XLA Ops:
  6.5 49.1 %copy-start = (f32[16,127]{1,0:T(8,128)S(1)}, f32[16,127]{1,0:T(8,128)}, u32[]{:S(2)}) copy-start(f32[16,127]{1,0:T(8,128)} %param.9) | copy-start | bytes 24388
  8.1 36.4 %copy-start.7 = (bf16[128,3072]{1,0:T(8,128)(2,1)S(1)}, bf16[128,3072]{1,0:T(8,128)(2,1)}, u32[]{:S(2)}) copy-start(bf16[128,3072]{1,0:T(8,128)(2,1)} %param.7) | copy-start | bytes 2359300
  47.9 6.0 %copy-start.9 = (f32[16,15]{1,0:T(8,128)S(1)}, f32[16,15]{1,0:T(8,128)}, u32[]{:S(2)}) copy-start(f32[16,15]{1,0:T(8,128)} %param.10) | copy-start | bytes 2884
  47.9 6.3 %copy-start.10 = (f32[16,15]{1,0:T(8,128)S(1)}, f32[16,15]{1,0:T(8,128)}, u32[]{:S(2)}) copy-start(f32[16,15]{1,0:T(8,128)} %param.11) | copy-start | bytes 2884
  47.9 167.4 %all-to-all-start = ((bf16[8,128,3072]{2,1,0:T(8,128)(2,1)}), bf16[8,128,3072]{2,1,0:T(8,128)(2,1)}, u32[]{:S(2)}, u32[]{:S(2)}) async-start(bf16[8,128,3072]{2,1,0:T(8,128)(2,1)} %stack.2), calls=%async_computation | async-start | bytes 12582912 | tf_op jit(solution)/shard_map/all_to_all | solution.py:67
  52.8 243.8 %all-gather.2.cloned.1.call-start = ((), (), s32[]{:S(2)}) async-start(), calls=%async_computation.5 | async-start | bytes 2359296 | tf_op jit(solution)/shard_map/all_gather | solution.py:95
  53.6 6.3 %copy-start.2 = (bf16[2,64,1,2,1024]{4,3,2,1,0:T(2,128)(2,1)S(1)}, bf16[2,64,1,2,1024]{4,3,2,1,0:T(2,128)(2,1)}, u32[]{:S(2)}) copy-start(bf16[2,64,1,2,1024]{4,3,2,1,0:T(2,128)(2,1)} %param.6) | copy-start | bytes 1572868
  247.5 26.4 %all-to-all-start.4 = ((bf16[2,16,1,8,1024]{4,1,0,2,3:T(8,128)(2,1)}), bf16[2,16,1,8,1024]{4,1,0,2,3:T(8,128)(2,1)}, u32[]{:S(2)}, u32[]{:S(2)}) async-start(bf16[2,16,1,8,1024]{4,1,0,2,3:T(8,128)(2,1)} %reshape.204), calls=%async_computation.4 | async-start | bytes 1048576 | tf_op jit(solution)/shard_map/all_to_all | solution.py:59
  254.1 3.4 %copy-start.8 = (bf16[256,1024]{1,0:T(8,128)(2,1)S(1)}, bf16[256,1024]{1,0:T(8,128)(2,1)}, u32[]{:S(2)}) copy-start(bf16[256,1024]{1,0:T(8,128)(2,1)} %reshape.182) | copy-start | bytes 1572868
  257.6 5.9 %copy-start.6 = (bf16[2,8,8,2,1,16,64]{6,5,4,3,2,1,0:T(8,128)(2,1)S(1)}, bf16[2,8,8,2,1,16,64]{6,5,4,3,2,1,0:T(8,128)(2,1)}, u32[]{:S(2)}) copy-start(bf16[2,8,8,2,1,16,64]{6,5,4,3,2,1,0:T(8,128)(2,1)} %get-tuple-element.5) | copy-start | bytes 1572868
  271.6 6.8 %copy-start.4 = (bf16[2,64,1,2,1,16,64]{6,5,4,3,1,0,2:T(8,128)(2,1)S(1)}, bf16[2,64,1,2,1,16,64]{6,5,4,3,1,0,2:T(8,128)(2,1)}, u32[]{:S(2)}) copy-start(bf16[2,64,1,2,1,16,64]{6,5,4,3,1,0,2:T(8,128)(2,1)} %get-tuple-element.9) | copy-start | bytes 1572868
  271.6 6.8 %copy-start.5 = (bf16[2,64,1,2,1,16,64]{6,5,4,3,1,0,2:T(8,128)(2,1)S(1)}, bf16[2,64,1,2,1,16,64]{6,5,4,3,1,0,2:T(8,128)(2,1)}, u32[]{:S(2)}) copy-start(bf16[2,64,1,2,1,16,64]{6,5,4,3,1,0,2:T(8,128)(2,1)} %get-tuple-element.10) | copy-start | bytes 1572868
  273.9 19.3 %all-to-all-start.2 = ((bf16[2,8,8,2,1024]{4,3,1,0,2:T(2,128)(2,1)}), bf16[2,8,8,2,1024]{4,3,1,0,2:T(2,128)(2,1)}, u32[]{:S(2)}, u32[]{:S(2)}) async-start(bf16[2,8,8,2,1024]{4,3,1,0,2:T(2,128)(2,1)} %reshape.203), calls=%async_computation.2 | async-start | bytes 1048576 | tf_op jit(solution)/shard_map/all_to_all | solution.py:55
  294.7 1.8 copy-start.3
  296.6 4.1 %copy-start.1 = (f32[16,127]{1,0:T(8,128)S(1)}, f32[16,127]{1,0:T(8,128)}, u32[]{:S(2)}) copy-start(f32[16,127]{1,0:T(8,128)} %param.9) | copy-start | bytes 24388
Sparse Core Ops, SparseCore 0:
  55.8 135.6 all-gather.1
